TPU v7x, 32 devices: a whole 2x2x4 slice. The times are simulated.
32 devices in a mesh: gx: 4 (over y, core), gy: 8 (over z, x).
Axes of the slice: x: 2, y: 2, z: 4, core: 2. Of those that a mesh axis runs over, the one named last changes fastest.
Arguments:
- pool_old: float32 [40, 131072], P(None, ('gx', 'gy')), may hold values from 0.5 to 2
- pool_new: float32 [40, 131072], P(None, ('gx', 'gy')), may hold values from 0.5 to 2
- flux: float32 [40, 131072], P(None, ('gx', 'gy')), may hold values from -6 to 6
- area: float32 [131072], P(('gx', 'gy')), may hold values from 0.05 to 1
- pft_id: int32 [131072], P(('gx', 'gy')), may hold values from 0 to 78
- region_id: int32 [131072], P(('gx', 'gy')), may hold values from 0 to 31, as said below
Outputs:
- pool_totals: float32 [40, 2528], replicated
- error_totals: float32 [40, 2528], replicated
Inputs may be any that keep to these rules, and one draw needn't show every extreme that they name: `region_id`: patch i lies in block k = i // 4096; with K = 32 blocks, its region is (k * 32) // K or ((k * 32) // K + 1) mod 32.
All inputs are finite; a program needn't handle non-finite values.
Results may differ from a plain program's by a relative error of at most 0.000076.
Values sent between devices are 32-bit elements; how exact they have to be, the bound alone decides.
No kernel may reach another device: no remote copies, remote signals or barrier semaphores. Data moves between devices by JAX's collectives and lax.ppermute only.
A program may use at most 64 MiB of HBM per device.

v0:
```python
import jax
import jax.numpy as jnp
from jax import lax
from jax.sharding import PartitionSpec as P

POOLS = 40
PFT = 79
REGION = 32
CELLS = 2528


def shards(pool_old, pool_new, flux, area, pft_id, region_id):
    width_x = lax.axis_size("gx")
    width_y = lax.axis_size("gy")
    devices_all = width_x * width_y
    position = lax.axis_index("gx") * width_y + lax.axis_index("gy")
    base = position * REGION // devices_all
    offset_here = (region_id - base) % REGION
    compact_cell = pft_id * 2 + offset_here
    stored = area[None, :] * pool_new
    balance = area[None, :] * (pool_new - pool_old - 0.5 * flux)
    stacked = jnp.concatenate([stored, balance], axis=0)
    rows = stacked.shape[0]
    patch_count = stacked.shape[1]
    block = min(512, patch_count)
    blocks = patch_count // block
    stacked_blocks = stacked.reshape(rows, blocks, block).transpose(1, 0, 2)
    cell_blocks = compact_cell.reshape(blocks, block)
    columns = jnp.arange(2 * PFT, dtype=jnp.int32)

    def accumulate(totals, inputs):
        values, cells_here = inputs
        onehot = (cells_here[:, None] == columns[None, :]).astype(jnp.float32)
        added = jnp.dot(
            values, onehot, preferred_element_type=jnp.float32, precision=lax.Precision.HIGHEST
        )
        return (totals + added, None)

    local_table, _ = lax.scan(
        accumulate, jnp.zeros((rows, 2 * PFT), jnp.float32), (stacked_blocks, cell_blocks)
    )
    local_table = local_table.reshape(rows, PFT, 2)
    region_axis = jnp.arange(REGION, dtype=jnp.int32)
    pair_axis = jnp.arange(2, dtype=jnp.int32)
    span = REGION // width_x + 1
    start = lax.axis_index("gx") * (REGION // width_x)
    span_axis = jnp.arange(span, dtype=jnp.int32)
    into_group = ((base - start + pair_axis)[:, None] == span_axis[None, :]).astype(jnp.float32)
    group_table = jnp.einsum(
        "apj,jw->apw", local_table, into_group, precision=lax.Precision.HIGHEST
    )
    group_total = lax.psum(group_table, "gy")
    into_full = (((start + span_axis) % REGION)[:, None] == region_axis[None, :]).astype(
        jnp.float32
    )
    placed = jnp.einsum("apw,wr->apr", group_total, into_full, precision=lax.Precision.HIGHEST)
    totals = lax.psum(placed.reshape(rows, CELLS), "gx")
    patch_all = patch_count * devices_all
    totals = totals * jnp.float32(CELLS / patch_all)
    return (totals[:POOLS], totals[POOLS:])


def solution(mesh):
    return jax.shard_map(
        shards,
        mesh=mesh,
        in_specs=(
            P(None, ("gx", "gy")),
            P(None, ("gx", "gy")),
            P(None, ("gx", "gy")),
            P(("gx", "gy")),
            P(("gx", "gy")),
            P(("gx", "gy")),
        ),
        out_specs=(P(), P()),
        check_vma=False,
    )
```

profile of v0, /device:TPU:0, one launch (start us, length us, event | category | flops | bytes accessed | tf_op | source)
XLA Modules:
  0.0 140.4 jit_solution(4403642553132659175)
XLA Ops:
  7.2 0.8 fusion.4
  8.0 1.6 %broadcast_multiply_fusion.1 = (f32[40,4096]{1,0:T(8,128)S(1)}, f32[40,4096]{1,0:T(8,128)S(1)}) fusion(f32[40,4096]{1,0:T(8,128)} %param.9, f32[4096]{0:T(1024)} %param.11, f32[40,4096]{1,0:T(8,128)} %param.10, f32[40,4096]{1,0:T(8,128)} %param.8), kind=kLoop, calls=%fused_computation.10 | loop fusion | flops 819200 | bytes 3293184 | tf_op jit(solution)/shard_map/mul | solution.py:20
  9.7 0.8 copy.13
  10.6 4.8 %while.11 = (s32[]{:T(128)}, f32[80,158]{1,0:T(8,128)S(1)}, f32[8,80,512]{2,0,1:T(8,128)S(1)}, s32[8,512]{1,0:T(8,128)S(1)}, s32[]{:T(128)}, /*index=5*/s32[]{:T(128)}) while((s32[]{:T(128)}, f32[80,158]{1,0:T(8,128)S(1)}, f32[8,80,512]{2,0,1:T(8,128)S(1)}, s32[8,512]{1,0:T(8,128)S(1)}, s32[]{:T(128)}, /*index=5*/s32[]{:T(128)}) %tuple.36), condition=%wide.region_1.2_spmd.clone, body=%wide.region_0.1_spmd.clone.sunk | while | flops 77766336 | bytes 598871 | solution.py:39
  10.6 0.1 constant_dynamic-slice_fusion.5
  10.8 0.4 convolution_add_fusion.2
  11.2 0.1 constant_dynamic-slice_fusion.5
  11.4 0.4 convolution_add_fusion.2
  11.8 0.1 constant_dynamic-slice_fusion.5
  12.0 0.4 convolution_add_fusion.2
  12.4 0.1 constant_dynamic-slice_fusion.5
  12.5 0.4 convolution_add_fusion.2
  13.0 0.1 constant_dynamic-slice_fusion.5
  13.1 0.4 convolution_add_fusion.2
  13.7 0.4 convolution_add_fusion.2
  14.3 0.4 convolution_add_fusion.2
  14.9 0.4 convolution_add_fusion.2
  15.5 1.4 fusion.9
  17.0 76.4 %all-reduce.3.cloned.1.call-done = f32[80,79,9]{0,2,1:T(8,128)} async-done(((f32[80,79,9]{0,2,1:T(8,128)}), f32[80,79,9]{0,2,1:T(8,128)}) %all-reduce.3.cloned.1.call-update) | async-done | bytes 227536 | tf_op jit(solution)/shard_map/psum | solution.py:52
  93.4 1.9 %fusion.6 = f32[80,79,32]{0,2,1:T(8,128)S(1)} fusion(f32[80,79,9]{0,2,1:T(8,128)} %all-reduce.3.cloned.1.call-done, s32[9]{0:T(128)S(1)} %and_select_fusion), kind=kOutput, calls=%fused_computation.18 | convolution fusion | flops 21842208 | bytes 1036516 | tf_op jit(solution)/shard_map/apw,wr->apr/dot_general | solution.py:56
  95.3 1.3 copy.11
  96.6 34.8 %all-reduce.5.cloned.1.call-done = f32[80,2528]{1,0:T(8,128)} async-done(((f32[80,2528]{1,0:T(8,128)}), f32[80,2528]{1,0:T(8,128)}) %all-reduce.5.cloned.1.call-update) | async-done | bytes 808976 | tf_op jit(solution)/shard_map/psum | solution.py:57
  131.4 1.2 broadcast_multiply_fusion
  132.7 0.9 fusion.15
  (22 shorter events, 0.9 us)
Async XLA Ops:
  7.2 86.3 %all-reduce.3.cloned.1.call-start = ((), (), s32[]{:S(2)}) async-start(), calls=%async_computation | async-start | bytes 1294336 | tf_op jit(solution)/shard_map/psum | solution.py:52
  16.9 114.5 %all-reduce.5.cloned.1.call-start = ((), (), s32[]{:S(2)}) async-start(), calls=%async_computation.1 | async-start | bytes 1638400 | tf_op jit(solution)/shard_map/psum | solution.py:57
Sparse Core Ops, SparseCore 0:
  17.0 76.3 all-reduce.2
  96.7 34.6 all-reduce.4
where the time goes:
time: 141 us; the launch traced here: 140 us
  waiting for transfers between devices  111 us (79%)
  between operations  14.1 us (10%)
  matrix products  6.42 us (5%)
  local copies, waits for them, and re-layouts  4.48 us (3%)
  other arithmetic  3.68 us (3%)
    psum x1, waiting for transfers between devices, shards(): group_total = lax.psum(group_table, 'gy')  76.4 us
    psum x1, waiting for transfers between devices, shards(): totals = lax.psum(placed.reshape(rows, CELLS), 'gx')  34.8 us
    dot_general x8, matrix products, accumulate(): jnp.dot(values, onehot, preferred_element_type=jnp.float32, precision=lax...  3.17 us
  transfers between devices with their start and end apart: 2, of which 2 were waited for; matrix products, arithmetic and copies ran while one was open for 0% of the time, Pallas kernels for 0%

commit v1 on v0

v1 whole, which is shorter than its diff:
```python
import functools

import jax
import jax.numpy as jnp
from jax import lax
from jax.experimental import pallas as pl
from jax.experimental.pallas import tpu as pltpu
from jax.sharding import PartitionSpec as P

POOLS = 40
PFT = 79
REGION = 32
CELLS = 2528
GROUP = 28
GROUPS = 3
ROWS = 2 * GROUP
LANES = 128
AXES = ("gx", "gy")


def table_kernel(scale, base_ref, old_ref, new_ref, flux_ref, area_ref, pft_ref, region_ref, out_ref, acc_ref):
    step = pl.program_id(0)

    @pl.when(step == 0)
    def _():
        acc_ref[...] = jnp.zeros_like(acc_ref)

    area = area_ref[...]
    new = new_ref[...]
    stored = area * new
    balance = area * (new - old_ref[...] - 0.5 * flux_ref[...])
    values = jnp.concatenate([stored, balance], axis=0)
    high = values.astype(jnp.bfloat16)
    rest = values - high.astype(jnp.float32)
    middle = rest.astype(jnp.bfloat16)
    low = (rest - middle.astype(jnp.float32)).astype(jnp.bfloat16)
    parts = jnp.concatenate([high, middle, low], axis=0)
    pft = pft_ref[...]
    group = (pft >= GROUP).astype(jnp.int32) + (pft >= 2 * GROUP).astype(jnp.int32)
    here = (region_ref[...] != base_ref[0]).astype(jnp.int32)
    cell = here * 96 + group * (32 - GROUP) + pft
    rows = lax.broadcasted_iota(jnp.int32, (192, cell.shape[1]), 0)
    onehot = (rows == cell).astype(jnp.bfloat16)
    acc_ref[...] += lax.dot_general(
        onehot, parts, (((1,), (1,)), ((), ())), preferred_element_type=jnp.float32
    )

    @pl.when(step == pl.num_programs(0) - 1)
    def _():
        both = 2 * POOLS
        total = acc_ref[...]
        total = (total[:, :both] + total[:, both : 2 * both] + total[:, 2 * both : 3 * both]) * scale
        for j in range(2):
            for s in range(2):
                pieces = [
                    total[j * 96 + g * 32 : j * 96 + g * 32 + GROUP, s * POOLS : (s + 1) * POOLS]
                    for g in range(GROUPS)
                ]
                pieces.append(jnp.zeros((GROUP, LANES - GROUPS * POOLS), jnp.float32))
                out_ref[j, s * GROUP : (s + 1) * GROUP, :] = jnp.concatenate(pieces, axis=1)


def local_tables(scale, base, pool_old, pool_new, flux, area, pft_id, region_id):
    patches = area.shape[0]
    chunk = min(1024, patches)
    wide = pl.BlockSpec((POOLS, chunk), lambda k: (0, k))
    narrow = pl.BlockSpec((1, chunk), lambda k: (0, k))
    return pl.pallas_call(
        functools.partial(table_kernel, scale),
        grid=(patches // chunk,),
        out_shape=jax.ShapeDtypeStruct((2, ROWS, LANES), jnp.float32),
        in_specs=[pl.BlockSpec(memory_space=pltpu.SMEM), wide, wide, wide, narrow, narrow, narrow],
        out_specs=pl.BlockSpec((2, ROWS, LANES), lambda k: (0, 0, 0)),
        scratch_shapes=[pltpu.VMEM((192, 240), jnp.float32)],
        name="local_tables",
    )(
        base.reshape(1),
        pool_old,
        pool_new,
        flux,
        area.reshape(1, patches),
        pft_id.reshape(1, patches),
        region_id.reshape(1, patches),
    )


def assemble_kernel(table_ref, stored_ref, balance_ref):
    for s, out_ref in enumerate((stored_ref, balance_ref)):
        for quad in range(GROUP // 4):
            block = jnp.concatenate(
                [table_ref[pl.ds(s * GROUP + quad * 4 + i, REGION, stride=ROWS), :] for i in range(4)],
                axis=0,
            ).T
            for g in range(GROUPS):
                column = (g * (GROUP // 4) + quad) * LANES
                width = min(LANES, CELLS - column)
                if width > 0:
                    out_ref[:, column : column + width] = block[g * POOLS : (g + 1) * POOLS, :width]


def assemble(tables):
    return pl.pallas_call(
        assemble_kernel,
        out_shape=[jax.ShapeDtypeStruct((POOLS, CELLS), jnp.float32)] * 2,
        name="assemble",
    )(tables.reshape(REGION * ROWS, LANES))


def join(low, high, axis):
    count = low.shape[axis]
    cut = lambda table, first, last: lax.slice_in_dim(table, first, last, axis=axis)
    return jnp.concatenate(
        [cut(low, 0, count - 1), cut(low, count - 1, count) + cut(high, 0, 1), cut(high, 1, count)],
        axis=axis,
    )


def gather_regions(tables, position, width_x, width_y):
    devices = width_x * width_y

    def exchange(mine, step):
        other = lax.ppermute(mine, AXES, [(i, i ^ step) for i in range(devices)])
        lower = (position // step) % 2 == 0
        return jnp.where(lower, mine, other), jnp.where(lower, other, mine)

    step = 1
    while step < width_y:
        tables = join(*exchange(tables, step), 0)
        step *= 2
    tables = tables[None]
    step = devices // 2
    while step >= width_y:
        tables = jnp.stack(exchange(tables, step), axis=1)
        tables = tables.reshape(-1, *tables.shape[2:])
        step //= 2
    while tables.shape[0] > 1:
        tables = join(tables[0::2], tables[1::2], 1)
    tables = tables[0]
    return jnp.concatenate([tables[:1] + tables[-1:], tables[1:-1]], axis=0)


def shards(pool_old, pool_new, flux, area, pft_id, region_id):
    width_x = lax.axis_size("gx")
    width_y = lax.axis_size("gy")
    devices = width_x * width_y
    position = lax.axis_index("gx") * width_y + lax.axis_index("gy")
    base = position * REGION // devices
    scale = CELLS / (area.shape[0] * devices)
    tables = local_tables(scale, base, pool_old, pool_new, flux, area, pft_id, region_id)
    if devices == REGION and width_x & (width_x - 1) == 0:
        tables = gather_regions(tables, position, width_x, width_y)
    else:
        here = (base + jnp.arange(2, dtype=jnp.int32)) % REGION
        spread = jnp.zeros((REGION, ROWS, LANES), jnp.float32).at[here].add(tables)
        tables = lax.psum(lax.psum(spread, "gy"), "gx")
    return tuple(assemble(tables))


def solution(mesh):
    return jax.shard_map(
        shards,
        mesh=mesh,
        in_specs=(
            P(None, ("gx", "gy")),
            P(None, ("gx", "gy")),
            P(None, ("gx", "gy")),
            P(("gx", "gy")),
            P(("gx", "gy")),
            P(("gx", "gy")),
        ),
        out_specs=(P(), P()),
        check_vma=False,
    )
```

time: 141 us -> 36.1 us (0.26)
  waiting for transfers between devices: 111 us -> 15.8 us
  between operations: 14.1 us -> 0.83 us
  starting transfers between devices: 0.08 us -> 10.2 us
  Pallas kernels: 0 us -> 6.49 us
  matrix products: 6.42 us -> 0 us
  local copies, waits for them, and re-layouts: 4.48 us -> 0.23 us
  other arithmetic: 3.68 us -> 2.26 us
    psum x2 -> x0, waiting for transfers between devices: 111 us -> none  [the longest x1 76.4 us: shards(): group_total = lax.psum(group_table, 'gy')]
    ppermute x0 -> x5, waiting for transfers between devices: none -> 15.8 us  [exchange(): other = lax.ppermute(mine, AXES, [(i, i ^ step) for i in range(devices)])]
    ppermute x0 -> x5, starting transfers between devices: none -> 10.2 us  [exchange(): other = lax.ppermute(mine, AXES, [(i, i ^ step) for i in range(devices)])]
    pallas_call x0 -> x2, Pallas kernels: none -> 6.49 us  [the longest x1 4.23 us: local_tables(): pl.pallas_call(functools.partial(table_kernel, scale), grid=(patches // c...]
    dot_general x10 -> x0, matrix products: 6.42 us -> none  [the longest x8 3.17 us: accumulate(): jnp.dot(values, onehot, preferred_element_type=jnp.float32, precision=lax...]
    mul x2 -> x0, other arithmetic: 2.82 us -> none  [the longest x1 1.62 us: shards(): stored = area[None, :] * pool_new]
  transfers between devices with their start and end apart: 2 -> 5, of which waited for: 2 -> 5; matrix products, arithmetic and copies ran while one was open for 0% -> 0% of each run, Pallas kernels for 0% -> 0%
where the time goes in v1:
time: 36.1 us; the launch traced here: 35.8 us
  waiting for transfers between devices  15.8 us (44%)
  starting transfers between devices  10.2 us (28%)
  Pallas kernels  6.49 us (18%)
  other arithmetic  2.26 us (6%)
  between operations  0.83 us (2%)
    ppermute x5, waiting for transfers between devices, exchange(): other = lax.ppermute(mine, AXES, [(i, i ^ step) for i in range(devices)])  15.8 us
    ppermute x5, starting transfers between devices, exchange(): other = lax.ppermute(mine, AXES, [(i, i ^ step) for i in range(devices)])  10.2 us
    pallas_call x1, Pallas kernels, local_tables(): pl.pallas_call(functools.partial(table_kernel, scale), grid=(patches // c...  4.23 us
    pallas_call x1, Pallas kernels, assemble(): pl.pallas_call(assemble_kernel, out_shape=[jax.ShapeDtypeStruct((POOLS, C...  2.26 us
    concatenate x1, other arithmetic, gather_regions(): return jnp.concatenate([tables[:1] + tables[-1:], tables[1:-1]], axis=0)  0.98 us
    select_n x3, other arithmetic, exchange(): return (jnp.where(lower, mine, other), jnp.where(lower, other, mine))  0.87 us
  transfers between devices with their start and end apart: 5, of which 5 were waited for; matrix products, arithmetic and copies ran while one was open for 0% of the time, Pallas kernels for 0%

profile of v1, /device:TPU:0, one launch (start us, length us, event | category | flops | bytes accessed | tf_op | source)
XLA Modules:
  0.0 35.8 jit_solution(8694758495427706110)
XLA Ops:
  0.6 4.2 %local_tables.1 = f32[2,56,128]{2,1,0:T(8,128)} custom-call(s32[1]{0:T(128)} %bitcast.base_ref, f32[40,4096]{1,0:T(8,128)} %old_ref.1, f32[40,4096]{1,0:T(8,128)} %new_ref.1, f32[40,4096]{1,0:T(8,128)} %flux_ref.1, f32[1,4096]{1,0:T(1,128)} %bitcast.32, s32[1,4096]{1,0:T(1,128)} %bitcast.33, s32[1,4096]{1,0:T(1,128)} %bitcast.34), custom_call_target="tpu_custom_call" | custom-call | tf_op jit(solution)/shard_map/local_tables/pallas_call | solution.py:68
  4.9 3.0 %collective-permute-start = (f32[2,56,128]{2,1,0:T(8,128)}, f32[2,56,128]{2,1,0:T(8,128)S(1)}, u32[]{:S(2)}, u32[]{:S(2)}) collective-permute-start(f32[2,56,128]{2,1,0:T(8,128)} %local_tables.1), channel_id=1, source_target_pairs={{0,1},{1,0},{2,3},{3,2},{4,5},{5,4},{6,7},{7,6},{8,9},{9,8},{10,11... | collective-permute-start | bytes 172040 | tf_op jit(solution)/shard_map/ppermute | solution.py:122
  7.9 2.4 %collective-permute-done = f32[2,56,128]{2,1,0:T(8,128)S(1)} collective-permute-done((f32[2,56,128]{2,1,0:T(8,128)}, f32[2,56,128]{2,1,0:T(8,128)S(1)}, u32[]{:S(2)}, u32[]{:S(2)}) %collective-permute-start) | collective-permute-done | bytes 57376 | tf_op jit(solution)/shard_map/ppermute | solution.py:122
  10.2 0.8 %broadcast_select_fusion.5 = (f32[2,56,128]{2,1,0:T(8,128)S(1)}, f32[2,56,128]{2,1,0:T(8,128)S(1)}) fusion(f32[2,56,128]{2,1,0:T(8,128)} %local_tables.1, f32[2,56,128]{2,1,0:T(8,128)S(1)} %collective-permute-done, pred[]{:T(512)S(6)} %eq.25), kind=kLoop, calls=%fused_computation.34 | loop fusion | flops 28672 | bytes 229377 | tf_op jit(solution)/shard_map/jit(_where)/select_n | solution.py:124
  11.1 2.2 %collective-permute-start.1 = (f32[3,56,128]{2,1,0:T(8,128)S(1)}, f32[3,56,128]{2,1,0:T(8,128)S(1)}, u32[]{:S(2)}, u32[]{:S(2)}) collective-permute-start(f32[3,56,128]{2,1,0:T(8,128)S(1)} %pad_maximum_fusion.7), channel_id=1, source_target_pairs={{0,2},{1,3},{2,0},{3,1},{4,6},{5,7},{6,4},{7,5},{8,10},{9,11},{10,... | collective-permute-start | bytes 258056 | tf_op jit(solution)/shard_map/ppermute | solution.py:122
  13.3 2.5 %collective-permute-done.1 = f32[3,56,128]{2,1,0:T(8,128)S(1)} collective-permute-done((f32[3,56,128]{2,1,0:T(8,128)S(1)}, f32[3,56,128]{2,1,0:T(8,128)S(1)}, u32[]{:S(2)}, u32[]{:S(2)}) %collective-permute-start.1) | collective-permute-done | bytes 86048 | tf_op jit(solution)/shard_map/ppermute | solution.py:122
  15.8 3.1 %collective-permute-start.2 = (f32[5,56,128]{2,1,0:T(8,128)S(1)}, f32[5,56,128]{2,1,0:T(8,128)S(1)}, u32[]{:S(2)}, u32[]{:S(2)}) collective-permute-start(f32[5,56,128]{2,1,0:T(8,128)S(1)} %pad_maximum_fusion.6), channel_id=1, source_target_pairs={{0,4},{1,5},{2,6},{3,7},{4,0},{5,1},{6,2},{7,3},{8,12},{9,13},{10,... | collective-permute-start | bytes 430088 | tf_op jit(solution)/shard_map/ppermute | solution.py:122
  18.9 4.6 %collective-permute-done.2 = f32[5,56,128]{2,1,0:T(8,128)S(1)} collective-permute-done((f32[5,56,128]{2,1,0:T(8,128)S(1)}, f32[5,56,128]{2,1,0:T(8,128)S(1)}, u32[]{:S(2)}, u32[]{:S(2)}) %collective-permute-start.2) | collective-permute-done | bytes 143392 | tf_op jit(solution)/shard_map/ppermute | solution.py:122
  23.6 1.9 %collective-permute-start.3 = (f32[1,9,56,128]{3,2,1,0:T(8,128)S(1)}, f32[1,9,56,128]{3,2,1,0:T(8,128)S(1)}, u32[]{:S(2)}, u32[]{:S(2)}) collective-permute-start(f32[1,9,56,128]{3,2,1,0:T(8,128)S(1)} %maximum_bitcast_fusion.1), channel_id=1, source_target_pairs={{0,16},{1,17},{2,18},{3,19},{4,20},{5,21},{6,22},{7,23},{8,24},{9,... | collective-permute-start | bytes 774152 | tf_op jit(solution)/shard_map/ppermute | solution.py:122
  25.5 4.5 %collective-permute-done.3 = f32[1,9,56,128]{3,2,1,0:T(8,128)S(1)} collective-permute-done((f32[1,9,56,128]{3,2,1,0:T(8,128)S(1)}, f32[1,9,56,128]{3,2,1,0:T(8,128)S(1)}, u32[]{:S(2)}, u32[]{:S(2)}) %collective-permute-start.3) | collective-permute-done | bytes 258080 | tf_op jit(solution)/shard_map/ppermute | solution.py:122
  30.1 0.1 maximum_bitcast_fusion
  30.1 0.1 collective-permute-start.4
  30.2 1.9 %collective-permute-done.4 = f32[2,9,56,128]{3,2,1,0:T(8,128)S(1)} collective-permute-done((f32[2,9,56,128]{3,2,1,0:T(8,128)S(1)}, f32[2,9,56,128]{3,2,1,0:T(8,128)S(1)}, u32[]{:S(2)}, u32[]{:S(2)}) %collective-permute-start.4) | collective-permute-done | bytes 516128 | tf_op jit(solution)/shard_map/ppermute | solution.py:122
  32.1 0.1 select_bitcast_fusion.1
  32.2 0.1 pad_maximum_fusion
  32.2 0.1 copy.8
  32.3 0.1 fusion.6
  32.5 0.1 fusion.1
  32.6 1.0 %pad_maximum_fusion.1 = f32[32,56,128]{2,1,0:T(8,128)} fusion(f32[31,56,128]{2,1,0:T(8,128)S(1)} %fusion.1, f32[1,56,128]{2,1,0:T(8,128)S(1)} %get-tuple-element.2), kind=kLoop, calls=%fused_computation.1 | loop fusion | flops 229376 | bytes 1835008 | tf_op jit(solution)/shard_map/concatenate | solution.py:139
  33.6 2.3 %assemble.1 = (f32[40,2528]{1,0:T(8,128)}, f32[40,2528]{1,0:T(8,128)}) custom-call(f32[1792,128]{1,0:T(8,128)} %bitcast.31), custom_call_target="tpu_custom_call" | custom-call | tf_op jit(solution)/shard_map/assemble/pallas_call | solution.py:102
  (17 shorter events, 0.3 us)
Async XLA Ops:
  4.9 5.3 %collective-permute-start = (f32[2,56,128]{2,1,0:T(8,128)}, f32[2,56,128]{2,1,0:T(8,128)S(1)}, u32[]{:S(2)}, u32[]{:S(2)}) collective-permute-start(f32[2,56,128]{2,1,0:T(8,128)} %local_tables.1), channel_id=1, source_target_pairs={{0,1},{1,0},{2,3},{3,2},{4,5},{5,4},{6,7},{7,6},{8,9},{9,8},{10,11... | collective-permute-start | bytes 172040 | tf_op jit(solution)/shard_map/ppermute | solution.py:122
  11.1 4.6 %collective-permute-start.1 = (f32[3,56,128]{2,1,0:T(8,128)S(1)}, f32[3,56,128]{2,1,0:T(8,128)S(1)}, u32[]{:S(2)}, u32[]{:S(2)}) collective-permute-start(f32[3,56,128]{2,1,0:T(8,128)S(1)} %pad_maximum_fusion.7), channel_id=1, source_target_pairs={{0,2},{1,3},{2,0},{3,1},{4,6},{5,7},{6,4},{7,5},{8,10},{9,11},{10,... | collective-permute-start | bytes 258056 | tf_op jit(solution)/shard_map/ppermute | solution.py:122
  15.8 7.7 %collective-permute-start.2 = (f32[5,56,128]{2,1,0:T(8,128)S(1)}, f32[5,56,128]{2,1,0:T(8,128)S(1)}, u32[]{:S(2)}, u32[]{:S(2)}) collective-permute-start(f32[5,56,128]{2,1,0:T(8,128)S(1)} %pad_maximum_fusion.6), channel_id=1, source_target_pairs={{0,4},{1,5},{2,6},{3,7},{4,0},{5,1},{6,2},{7,3},{8,12},{9,13},{10,... | collective-permute-start | bytes 430088 | tf_op jit(solution)/shard_map/ppermute | solution.py:122
  23.6 6.4 %collective-permute-start.3 = (f32[1,9,56,128]{3,2,1,0:T(8,128)S(1)}, f32[1,9,56,128]{3,2,1,0:T(8,128)S(1)}, u32[]{:S(2)}, u32[]{:S(2)}) collective-permute-start(f32[1,9,56,128]{3,2,1,0:T(8,128)S(1)} %maximum_bitcast_fusion.1), channel_id=1, source_target_pairs={{0,16},{1,17},{2,18},{3,19},{4,20},{5,21},{6,22},{7,23},{8,24},{9,... | collective-permute-start | bytes 774152 | tf_op jit(solution)/shard_map/ppermute | solution.py:122
  30.1 2.0 %collective-permute-start.4 = (f32[2,9,56,128]{3,2,1,0:T(8,128)S(1)}, f32[2,9,56,128]{3,2,1,0:T(8,128)S(1)}, u32[]{:S(2)}, u32[]{:S(2)}) collective-permute-start(f32[2,9,56,128]{3,2,1,0:T(8,128)S(1)} %maximum_bitcast_fusion), channel_id=1, source_target_pairs={{0,8},{1,9},{2,10},{3,11},{4,12},{5,13},{6,14},{7,15},{8,0},{9,1},... | collective-permute-start | bytes 1548296 | tf_op jit(solution)/shard_map/ppermute | solution.py:122

commit v2 on v0

v2 whole, which is shorter than its diff:
```python
import functools

import jax
import jax.numpy as jnp
from jax import lax
from jax.experimental import pallas as pl
from jax.experimental.pallas import tpu as pltpu
from jax.sharding import PartitionSpec as P

POOLS = 40
PFT = 79
REGION = 32
CELLS = 2528
GROUP = 28
GROUPS = 3
ROWS = 2 * GROUP
LANES = 128
HALVES = (32, 24)
SLOT = 32
PAIR = GROUPS * SLOT
AXES = ("gx", "gy")
MIB = 1 << 20


def table_kernel(
    scale, chunk, old_hbm, new_hbm, flux_hbm, area_hbm, pft_hbm, region_hbm,
    first_ref, second_ref, old_ref, new_ref, flux_ref, area_ref, pft_ref, region_ref, acc_ref, sems,
):
    patches = area_hbm.shape[1]
    width_y = lax.axis_size("gy")
    devices = lax.axis_size("gx") * width_y
    base = (lax.axis_index("gx") * width_y + lax.axis_index("gy")) * REGION // devices
    pairs = (
        (pft_hbm, pft_ref), (region_hbm, region_ref), (area_hbm, area_ref),
        (new_hbm, new_ref), (old_hbm, old_ref), (flux_hbm, flux_ref),
    )
    copies = []
    for k in range(patches // chunk):
        part = pl.ds(k * chunk, chunk)
        copies.append(
            [pltpu.make_async_copy(a.at[:, part], b.at[:, part], sems.at[n, k]) for n, (a, b) in enumerate(pairs)]
        )
        for copy in copies[-1]:
            copy.start()
    for k, started in enumerate(copies):
        part = pl.ds(k * chunk, chunk)
        for copy in started:
            copy.wait()
        pft = pft_ref[:, part]
        group = (pft >= GROUP).astype(jnp.int32) + (pft >= 2 * GROUP).astype(jnp.int32)
        here = (region_ref[:, part] != base).astype(jnp.int32)
        cell = here * PAIR + group * (SLOT - GROUP) + pft
        columns = lax.broadcasted_iota(jnp.int32, (2 * PAIR, chunk), 0)
        onehot = (columns == cell).astype(jnp.bfloat16)
        area = area_ref[:, part]
        new = new_ref[:, part]
        stored = area * new
        balance = area * (new - old_ref[:, part] - 0.5 * flux_ref[:, part])
        values = jnp.concatenate([stored, balance], axis=0)
        high = values.astype(jnp.bfloat16)
        rest = values - high.astype(jnp.float32)
        middle = rest.astype(jnp.bfloat16)
        low = (rest - middle.astype(jnp.float32)).astype(jnp.bfloat16)
        parts = jnp.concatenate([high, middle, low], axis=0)
        added = lax.dot_general(
            parts, onehot, (((1,), (1,)), ((), ())), preferred_element_type=jnp.float32
        )
        if k == 0:
            acc_ref[...] = added
        else:
            acc_ref[...] += added
    both = 2 * POOLS
    total = acc_ref[...]
    total = (total[:both] + total[both : 2 * both] + total[2 * both :]) * scale
    total = jnp.concatenate([total, jnp.zeros((LANES - both, 2 * PAIR), jnp.float32)], axis=0).T
    for j in range(2):
        table = []
        for s in range(2):
            pieces = [
                total[j * PAIR + g * SLOT : j * PAIR + g * SLOT + GROUP, s * POOLS : (s + 1) * POOLS]
                for g in range(GROUPS)
            ]
            pieces.append(jnp.zeros((GROUP, LANES - GROUPS * POOLS), jnp.float32))
            table.append(jnp.concatenate(pieces, axis=1))
        table = jnp.concatenate(table, axis=0)
        first_ref[j] = table[: HALVES[0]]
        second_ref[j] = table[HALVES[0] :]


def local_tables(scale, pool_old, pool_new, flux, area, pft_id, region_id):
    patches = area.shape[0]
    chunk = min(1024, patches)
    steps = patches // chunk
    wide = pltpu.VMEM((POOLS, patches), jnp.float32)
    return pl.pallas_call(
        functools.partial(table_kernel, scale, chunk),
        out_shape=[jax.ShapeDtypeStruct((2, rows, LANES), jnp.float32) for rows in HALVES],
        in_specs=[pl.BlockSpec(memory_space=pltpu.HBM)] * 6,
        out_specs=[pl.BlockSpec(memory_space=pltpu.VMEM)] * 2,
        scratch_shapes=[
            wide,
            wide,
            wide,
            pltpu.VMEM((1, patches), jnp.float32),
            pltpu.VMEM((1, patches), jnp.int32),
            pltpu.VMEM((1, patches), jnp.int32),
            pltpu.VMEM((6 * POOLS, 2 * PAIR), jnp.float32),
            pltpu.SemaphoreType.DMA((6, steps)),
        ],
        compiler_params=pltpu.CompilerParams(vmem_limit_bytes=16 * MIB),
        name="local_tables",
    )(
        *(
            pltpu.with_memory_space_constraint(operand, pltpu.HBM)
            for operand in (
                pool_old,
                pool_new,
                flux,
                area.reshape(1, patches),
                pft_id.reshape(1, patches),
                region_id.reshape(1, patches),
            )
        )
    )


def assemble_kernel(masks, span, half_rows, sources, *refs):
    count = len(masks)
    out_ref = refs[count * len(half_rows)]
    full_refs = refs[count * len(half_rows) + 1 :]
    me = lax.axis_index("gx") if count > 1 else 0
    for h, rows in enumerate(half_rows):
        full_ref = full_refs[h]
        for m, mask in enumerate(masks):
            full_ref[me ^ mask] = refs[h * count + m][...].reshape((span + 1) * rows, LANES)
        for r in range(count):
            full_ref[r, :rows] += full_ref[(r - 1) % count, span * rows :]
    for quad in range(GROUP // 4):
        block = []
        for i in range(4):
            h, row = sources[quad * 4 + i]
            rows = half_rows[h]
            block += [full_refs[h][r, pl.ds(row, span, stride=rows), :] for r in range(count)]
        block = jnp.concatenate(block, axis=0).T
        for g in range(GROUPS):
            column = (g * (GROUP // 4) + quad) * LANES
            width = min(LANES, CELLS - column)
            if width > 0:
                out_ref[:, column : column + width] = block[g * POOLS : (g + 1) * POOLS, :width]


def assemble(name, masks, halves, sources):
    half_rows = [pieces[0].shape[1] for pieces in halves]
    span = halves[0][0].shape[0] - 1
    pieces = [piece for half in halves for piece in half]
    return pl.pallas_call(
        functools.partial(assemble_kernel, masks, span, half_rows, sources),
        out_shape=jax.ShapeDtypeStruct((POOLS, CELLS), jnp.float32),
        in_specs=[pl.BlockSpec(memory_space=pltpu.VMEM)] * len(pieces),
        out_specs=pl.BlockSpec(memory_space=pltpu.VMEM),
        scratch_shapes=[
            pltpu.VMEM((len(masks), (span + 1) * rows, LANES), jnp.float32) for rows in half_rows
        ],
        compiler_params=pltpu.CompilerParams(vmem_limit_bytes=8 * MIB),
        name=name,
    )(*pieces)


def join(low, high):
    return jnp.concatenate([low[:-1], low[-1:] + high[:1], high[1:]], axis=0)


def gather_rows(halves, position, width_x, width_y):
    devices = width_x * width_y

    def send(mine, step):
        return lax.ppermute(mine, AXES, [(i, i ^ step) for i in range(devices)])

    step = 1
    while step < width_y:
        lower = (position // step) % 2 == 0
        others = [send(mine, step) for mine in halves]
        halves = [
            join(jnp.where(lower, mine, other), jnp.where(lower, other, mine))
            for mine, other in zip(halves, others)
        ]
        step *= 2
    masks = [0]
    halves = [[mine] for mine in halves]
    mask = width_x // 2
    while mask:
        masks = masks + [m ^ mask for m in masks]
        halves = [pieces + [send(piece, mask * width_y) for piece in pieces] for pieces in halves]
        mask //= 2
    return masks, halves


def shards(pool_old, pool_new, flux, area, pft_id, region_id):
    width_x = lax.axis_size("gx")
    width_y = lax.axis_size("gy")
    devices = width_x * width_y
    position = lax.axis_index("gx") * width_y + lax.axis_index("gy")
    scale = CELLS / (area.shape[0] * devices)
    halves = local_tables(scale, pool_old, pool_new, flux, area, pft_id, region_id)
    if devices == REGION and width_x & (width_x - 1) == 0:
        masks, halves = gather_rows(halves, position, width_x, width_y)
    else:
        here = (position * REGION // devices + jnp.arange(2, dtype=jnp.int32)) % REGION
        full = []
        for tables in halves:
            spread = jnp.zeros((REGION + 1, *tables.shape[1:]), jnp.float32).at[here].add(tables)
            full.append([lax.psum(lax.psum(spread, "gy"), "gx")])
        masks, halves = [0], full
    first = HALVES[0]
    stored = assemble("stored", masks, halves[:1], [(0, i) for i in range(GROUP)])
    balance = assemble(
        "balance",
        masks,
        halves,
        [(0, i) if i < first else (1, i - first) for i in range(GROUP, 2 * GROUP)],
    )
    return stored, balance


def solution(mesh):
    return jax.shard_map(
        shards,
        mesh=mesh,
        in_specs=(
            P(None, ("gx", "gy")),
            P(None, ("gx", "gy")),
            P(None, ("gx", "gy")),
            P(("gx", "gy")),
            P(("gx", "gy")),
            P(("gx", "gy")),
        ),
        out_specs=(P(), P()),
        check_vma=False,
    )
```

time: 141 us -> 30.7 us (0.22)
  waiting for transfers between devices: 111 us -> 9.77 us
  starting transfers between devices: 0.08 us -> 14.3 us
  between operations: 14.1 us -> 0.81 us
  matrix products: 6.42 us -> 0 us
  Pallas kernels: 0 us -> 5.43 us
  local copies, waits for them, and re-layouts: 4.48 us -> 0.04 us
  other arithmetic: 3.68 us -> 0.14 us
    psum x2 -> x0, waiting for transfers between devices: 111 us -> none  [the longest x1 76.4 us: shards(): group_total = lax.psum(group_table, 'gy')]
    ppermute x0 -> x12, starting transfers between devices: none -> 14.3 us  [send(): return lax.ppermute(mine, AXES, [(i, i ^ step) for i in range(devices)])]
    ppermute x0 -> x12, waiting for transfers between devices: none -> 9.77 us  [send(): return lax.ppermute(mine, AXES, [(i, i ^ step) for i in range(devices)])]
    dot_general x10 -> x0, matrix products: 6.42 us -> none  [the longest x8 3.17 us: accumulate(): jnp.dot(values, onehot, preferred_element_type=jnp.float32, precision=lax...]
    pallas_call x0 -> x3, Pallas kernels: none -> 5.43 us  [the longest x1 3.24 us: local_tables(): pl.pallas_call(functools.partial(table_kernel, scale, chunk), out_shape=[...]
    mul x2 -> x0, other arithmetic: 2.82 us -> none  [the longest x1 1.62 us: shards(): stored = area[None, :] * pool_new]
  transfers between devices with their start and end apart: 2 -> 12, of which waited for: 2 -> 7; matrix products, arithmetic and copies ran while one was open for 0% -> 0% of each run, Pallas kernels for 0% -> 4%
where the time goes in v2:
time: 30.7 us; the launch traced here: 30.5 us
  starting transfers between devices  14.3 us (47%)
  waiting for transfers between devices  9.77 us (32%)
  Pallas kernels  5.43 us (18%)
  between operations  0.81 us (3%)
    ppermute x12, starting transfers between devices, send(): return lax.ppermute(mine, AXES, [(i, i ^ step) for i in range(devices)])  14.3 us
    ppermute x12, waiting for transfers between devices, send(): return lax.ppermute(mine, AXES, [(i, i ^ step) for i in range(devices)])  9.77 us
    pallas_call x1, Pallas kernels, local_tables(): pl.pallas_call(functools.partial(table_kernel, scale, chunk), out_shape=[...  3.24 us
    pallas_call x2, Pallas kernels, assemble(): pl.pallas_call(functools.partial(assemble_kernel, masks, span, half_rows,...  2.2 us
  transfers between devices with their start and end apart: 12, of which 7 were waited for; matrix products, arithmetic and copies ran while one was open for 0% of the time, Pallas kernels for 4%

profile of v2, /device:TPU:0, one launch (start us, length us, event | category | flops | bytes accessed | tf_op | source)
XLA Modules:
  0.0 30.5 jit_solution(3350247416118717977)
XLA Ops:
  0.6 3.2 %local_tables.1 = (f32[2,32,128]{2,1,0:T(8,128)S(1)}, f32[2,24,128]{2,1,0:T(8,128)S(1)}) custom-call(f32[40,4096]{1,0:T(8,128)} %old_hbm.1, f32[40,4096]{1,0:T(8,128)} %new_hbm.1, f32[40,4096]{1,0:T(8,128)} %flux_hbm.1, f32[1,4096]{1,0:T(1,128)} %bitcast.3, s32[1,4096]{1,0:T(1,128)} %bitcast.4, s32[1,4096]{1,0:T(1,128)} %bitcast.5), custom_call_target="tpu_custom_call" | custom-call | tf_op jit(solution)/shard_map/local_tables/pallas_call | solution.py:95
  3.9 3.0 %collective-permute-start.6 = (f32[2,24,128]{2,1,0:T(8,128)S(1)}, f32[2,24,128]{2,1,0:T(8,128)S(1)}, u32[]{:S(2)}, u32[]{:S(2)}) collective-permute-start(f32[2,24,128]{2,1,0:T(8,128)S(1)} %get-tuple-element.5), channel_id=1, source_target_pairs={{0,1},{1,0},{2,3},{3,2},{4,5},{5,4},{6,7},{7,6},{8,9},{9,8},{10,11... | collective-permute-start | bytes 73736 | tf_op jit(solution)/shard_map/ppermute | solution.py:177
  6.9 0.1 collective-permute-start
  7.0 1.7 %collective-permute-done.6 = f32[2,24,128]{2,1,0:T(8,128)S(1)} collective-permute-done((f32[2,24,128]{2,1,0:T(8,128)S(1)}, f32[2,24,128]{2,1,0:T(8,128)S(1)}, u32[]{:S(2)}, u32[]{:S(2)}) %collective-permute-start.6) | collective-permute-done | bytes 24608 | tf_op jit(solution)/shard_map/ppermute | solution.py:177
  8.7 2.4 %collective-permute-start.7 = (f32[3,24,128]{2,1,0:T(8,128)S(1)}, f32[3,24,128]{2,1,0:T(8,128)S(1)}, u32[]{:S(2)}, u32[]{:S(2)}) collective-permute-start(f32[3,24,128]{2,1,0:T(8,128)S(1)} %pad_maximum_fusion.5), channel_id=1, source_target_pairs={{0,2},{1,3},{2,0},{3,1},{4,6},{5,7},{6,4},{7,5},{8,10},{9,11},{10,... | collective-permute-start | bytes 110600 | tf_op jit(solution)/shard_map/ppermute | solution.py:177
  11.1 1.4 %collective-permute-start.1 = (f32[3,32,128]{2,1,0:T(8,128)S(1)}, f32[3,32,128]{2,1,0:T(8,128)S(1)}, u32[]{:S(2)}, u32[]{:S(2)}) collective-permute-start(f32[3,32,128]{2,1,0:T(8,128)S(1)} %pad_maximum_fusion.4), channel_id=1, source_target_pairs={{0,2},{1,3},{2,0},{3,1},{4,6},{5,7},{6,4},{7,5},{8,10},{9,11},{10,... | collective-permute-start | bytes 147464 | tf_op jit(solution)/shard_map/ppermute | solution.py:177
  12.5 0.5 %collective-permute-done.7 = f32[3,24,128]{2,1,0:T(8,128)S(1)} collective-permute-done((f32[3,24,128]{2,1,0:T(8,128)S(1)}, f32[3,24,128]{2,1,0:T(8,128)S(1)}, u32[]{:S(2)}, u32[]{:S(2)}) %collective-permute-start.7) | collective-permute-done | bytes 36896 | tf_op jit(solution)/shard_map/ppermute | solution.py:177
  13.1 3.1 %collective-permute-start.8 = (f32[5,24,128]{2,1,0:T(8,128)S(1)}, f32[5,24,128]{2,1,0:T(8,128)S(1)}, u32[]{:S(2)}, u32[]{:S(2)}) collective-permute-start(f32[5,24,128]{2,1,0:T(8,128)S(1)} %pad_maximum_fusion.3), channel_id=1, source_target_pairs={{0,4},{1,5},{2,6},{3,7},{4,0},{5,1},{6,2},{7,3},{8,12},{9,13},{10,... | collective-permute-start | bytes 184328 | tf_op jit(solution)/shard_map/ppermute | solution.py:177
  16.2 0.0 collective-permute-done.1
  16.3 1.7 %collective-permute-start.2 = (f32[5,32,128]{2,1,0:T(8,128)S(1)}, f32[5,32,128]{2,1,0:T(8,128)S(1)}, u32[]{:S(2)}, u32[]{:S(2)}) collective-permute-start(f32[5,32,128]{2,1,0:T(8,128)S(1)} %pad_maximum_fusion.2), channel_id=1, source_target_pairs={{0,4},{1,5},{2,6},{3,7},{4,0},{5,1},{6,2},{7,3},{8,12},{9,13},{10,... | collective-permute-start | bytes 245768 | tf_op jit(solution)/shard_map/ppermute | solution.py:177
  18.0 2.1 %collective-permute-done.8 = f32[5,24,128]{2,1,0:T(8,128)S(1)} collective-permute-done((f32[5,24,128]{2,1,0:T(8,128)S(1)}, f32[5,24,128]{2,1,0:T(8,128)S(1)}, u32[]{:S(2)}, u32[]{:S(2)}) %collective-permute-start.8) | collective-permute-done | bytes 61472 | tf_op jit(solution)/shard_map/ppermute | solution.py:177
  20.1 1.5 %collective-permute-done.2 = f32[5,32,128]{2,1,0:T(8,128)S(1)} collective-permute-done((f32[5,32,128]{2,1,0:T(8,128)S(1)}, f32[5,32,128]{2,1,0:T(8,128)S(1)}, u32[]{:S(2)}, u32[]{:S(2)}) %collective-permute-start.2) | collective-permute-done | bytes 81952 | tf_op jit(solution)/shard_map/ppermute | solution.py:177
  21.8 1.6 %collective-permute-start.3 = (f32[9,32,128]{2,1,0:T(8,128)S(1)}, f32[9,32,128]{2,1,0:T(8,128)S(1)}, u32[]{:S(2)}, u32[]{:S(2)}) collective-permute-start(f32[9,32,128]{2,1,0:T(8,128)S(1)} %pad_maximum_fusion.refs_0_), channel_id=1, source_target_pairs={{0,16},{1,17},{2,18},{3,19},{4,20},{5,21},{6,22},{7,23},{8,24},{9,... | collective-permute-start | bytes 442376 | tf_op jit(solution)/shard_map/ppermute | solution.py:177
  23.4 0.6 %collective-permute-start.9 = (f32[9,24,128]{2,1,0:T(8,128)S(1)}, f32[9,24,128]{2,1,0:T(8,128)S(1)}, u32[]{:S(2)}, u32[]{:S(2)}) collective-permute-start(f32[9,24,128]{2,1,0:T(8,128)S(1)} %pad_maximum_fusion.1.refs_4_), channel_id=1, source_target_pairs={{0,16},{1,17},{2,18},{3,19},{4,20},{5,21},{6,22},{7,23},{8,24},{9,... | collective-permute-start | bytes 331784 | tf_op jit(solution)/shard_map/ppermute | solution.py:177
  23.9 0.0 collective-permute-start.4
  23.9 3.0 %collective-permute-done.3.refs_1_ = f32[9,32,128]{2,1,0:T(8,128)S(1)} collective-permute-done((f32[9,32,128]{2,1,0:T(8,128)S(1)}, f32[9,32,128]{2,1,0:T(8,128)S(1)}, u32[]{:S(2)}, u32[]{:S(2)}) %collective-permute-start.3) | collective-permute-done | bytes 147488 | tf_op jit(solution)/shard_map/ppermute | solution.py:177
  27.0 0.0 collective-permute-start.5
  27.0 0.5 %collective-permute-start.10 = (f32[9,24,128]{2,1,0:T(8,128)S(1)}, f32[9,24,128]{2,1,0:T(8,128)S(1)}, u32[]{:S(2)}, u32[]{:S(2)}) collective-permute-start(f32[9,24,128]{2,1,0:T(8,128)S(1)} %pad_maximum_fusion.1.refs_4_), channel_id=1, source_target_pairs={{0,8},{1,9},{2,10},{3,11},{4,12},{5,13},{6,14},{7,15},{8,0},{9,1},... | collective-permute-start | bytes 331784 | tf_op jit(solution)/shard_map/ppermute | solution.py:177
  27.5 0.7 %collective-permute-done.9.refs_5_ = f32[9,24,128]{2,1,0:T(8,128)S(1)} collective-permute-done((f32[9,24,128]{2,1,0:T(8,128)S(1)}, f32[9,24,128]{2,1,0:T(8,128)S(1)}, u32[]{:S(2)}, u32[]{:S(2)}) %collective-permute-start.9) | collective-permute-done | bytes 110624 | tf_op jit(solution)/shard_map/ppermute | solution.py:177
  28.2 0.0 collective-permute-start.11
  28.2 0.2 collective-permute-done.5.refs_3_
  28.3 1.1 %stored.1 = f32[40,2528]{1,0:T(8,128)} custom-call(f32[9,32,128]{2,1,0:T(8,128)S(1)} %pad_maximum_fusion.refs_0_, f32[9,32,128]{2,1,0:T(8,128)S(1)} %collective-permute-done.3.refs_1_, f32[9,32,128]{2,1,0:T(8,128)S(1)} %collective-permute-done.4.refs_2_, f32[9,32,128]{2,1,0:T(8,128)S(1)} %collective-permute-done.5.refs_3_), custom_call_target="tpu_custom_call" | custom-call | tf_op jit(solution)/shard_map/stored/pallas_call | solution.py:156
  29.5 0.0 collective-permute-done.10.refs_6_
  29.5 1.1 %balance.1 = f32[40,2528]{1,0:T(8,128)} custom-call(f32[9,32,128]{2,1,0:T(8,128)S(1)} %pad_maximum_fusion.refs_0_, f32[9,32,128]{2,1,0:T(8,128)S(1)} %collective-permute-done.3.refs_1_, f32[9,32,128]{2,1,0:T(8,128)S(1)} %collective-permute-done.4.refs_2_, f32[9,32,128]{2,1,0:T(8,128)S(1)} %collective-permute-done.5.refs_3_, ...), custom_call_target="tpu_custom_call" | custom-call | tf_op jit(solution)/shard_map/balance/pallas_call | solution.py:156
  (29 shorter events, 0.2 us)
Async XLA Ops:
  3.9 4.8 %collective-permute-start.6 = (f32[2,24,128]{2,1,0:T(8,128)S(1)}, f32[2,24,128]{2,1,0:T(8,128)S(1)}, u32[]{:S(2)}, u32[]{:S(2)}) collective-permute-start(f32[2,24,128]{2,1,0:T(8,128)S(1)} %get-tuple-element.5), channel_id=1, source_target_pairs={{0,1},{1,0},{2,3},{3,2},{4,5},{5,4},{6,7},{7,6},{8,9},{9,8},{10,11... | collective-permute-start | bytes 73736 | tf_op jit(solution)/shard_map/ppermute | solution.py:177
  6.9 4.2 %collective-permute-start = (f32[2,32,128]{2,1,0:T(8,128)S(1)}, f32[2,32,128]{2,1,0:T(8,128)S(1)}, u32[]{:S(2)}, u32[]{:S(2)}) collective-permute-start(f32[2,32,128]{2,1,0:T(8,128)S(1)} %get-tuple-element.4), channel_id=1, source_target_pairs={{0,1},{1,0},{2,3},{3,2},{4,5},{5,4},{6,7},{7,6},{8,9},{9,8},{10,11... | collective-permute-start | bytes 98312 | tf_op jit(solution)/shard_map/ppermute | solution.py:177
  8.7 4.3 %collective-permute-start.7 = (f32[3,24,128]{2,1,0:T(8,128)S(1)}, f32[3,24,128]{2,1,0:T(8,128)S(1)}, u32[]{:S(2)}, u32[]{:S(2)}) collective-permute-start(f32[3,24,128]{2,1,0:T(8,128)S(1)} %pad_maximum_fusion.5), channel_id=1, source_target_pairs={{0,2},{1,3},{2,0},{3,1},{4,6},{5,7},{6,4},{7,5},{8,10},{9,11},{10,... | collective-permute-start | bytes 110600 | tf_op jit(solution)/shard_map/ppermute | solution.py:177
  11.1 5.1 %collective-permute-start.1 = (f32[3,32,128]{2,1,0:T(8,128)S(1)}, f32[3,32,128]{2,1,0:T(8,128)S(1)}, u32[]{:S(2)}, u32[]{:S(2)}) collective-permute-start(f32[3,32,128]{2,1,0:T(8,128)S(1)} %pad_maximum_fusion.4), channel_id=1, source_target_pairs={{0,2},{1,3},{2,0},{3,1},{4,6},{5,7},{6,4},{7,5},{8,10},{9,11},{10,... | collective-permute-start | bytes 147464 | tf_op jit(solution)/shard_map/ppermute | solution.py:177
  13.1 7.0 %collective-permute-start.8 = (f32[5,24,128]{2,1,0:T(8,128)S(1)}, f32[5,24,128]{2,1,0:T(8,128)S(1)}, u32[]{:S(2)}, u32[]{:S(2)}) collective-permute-start(f32[5,24,128]{2,1,0:T(8,128)S(1)} %pad_maximum_fusion.3), channel_id=1, source_target_pairs={{0,4},{1,5},{2,6},{3,7},{4,0},{5,1},{6,2},{7,3},{8,12},{9,13},{10,... | collective-permute-start | bytes 184328 | tf_op jit(solution)/shard_map/ppermute | solution.py:177
  16.3 5.4 %collective-permute-start.2 = (f32[5,32,128]{2,1,0:T(8,128)S(1)}, f32[5,32,128]{2,1,0:T(8,128)S(1)}, u32[]{:S(2)}, u32[]{:S(2)}) collective-permute-start(f32[5,32,128]{2,1,0:T(8,128)S(1)} %pad_maximum_fusion.2), channel_id=1, source_target_pairs={{0,4},{1,5},{2,6},{3,7},{4,0},{5,1},{6,2},{7,3},{8,12},{9,13},{10,... | collective-permute-start | bytes 245768 | tf_op jit(solution)/shard_map/ppermute | solution.py:177
  21.8 5.2 %collective-permute-start.3 = (f32[9,32,128]{2,1,0:T(8,128)S(1)}, f32[9,32,128]{2,1,0:T(8,128)S(1)}, u32[]{:S(2)}, u32[]{:S(2)}) collective-permute-start(f32[9,32,128]{2,1,0:T(8,128)S(1)} %pad_maximum_fusion.refs_0_), channel_id=1, source_target_pairs={{0,16},{1,17},{2,18},{3,19},{4,20},{5,21},{6,22},{7,23},{8,24},{9,... | collective-permute-start | bytes 442376 | tf_op jit(solution)/shard_map/ppermute | solution.py:177
  23.4 4.8 %collective-permute-start.9 = (f32[9,24,128]{2,1,0:T(8,128)S(1)}, f32[9,24,128]{2,1,0:T(8,128)S(1)}, u32[]{:S(2)}, u32[]{:S(2)}) collective-permute-start(f32[9,24,128]{2,1,0:T(8,128)S(1)} %pad_maximum_fusion.1.refs_4_), channel_id=1, source_target_pairs={{0,16},{1,17},{2,18},{3,19},{4,20},{5,21},{6,22},{7,23},{8,24},{9,... | collective-permute-start | bytes 331784 | tf_op jit(solution)/shard_map/ppermute | solution.py:177
  23.9 4.2 %collective-permute-start.4 = (f32[9,32,128]{2,1,0:T(8,128)S(1)}, f32[9,32,128]{2,1,0:T(8,128)S(1)}, u32[]{:S(2)}, u32[]{:S(2)}) collective-permute-start(f32[9,32,128]{2,1,0:T(8,128)S(1)} %pad_maximum_fusion.refs_0_), channel_id=1, source_target_pairs={{0,8},{1,9},{2,10},{3,11},{4,12},{5,13},{6,14},{7,15},{8,0},{9,1},... | collective-permute-start | bytes 442376 | tf_op jit(solution)/shard_map/ppermute | solution.py:177
  27.0 1.4 %collective-permute-start.5 = (f32[9,32,128]{2,1,0:T(8,128)S(1)}, f32[9,32,128]{2,1,0:T(8,128)S(1)}, u32[]{:S(2)}, u32[]{:S(2)}) collective-permute-start(f32[9,32,128]{2,1,0:T(8,128)S(1)} %collective-permute-done.3.refs_1_), channel_id=1, source_target_pairs={{0,8},{1,9},{2,10},{3,11},{4,12},{5,13},{6,14},{7,15},{8,0},{9,1},... | collective-permute-start | bytes 442376 | tf_op jit(solution)/shard_map/ppermute | solution.py:177
  27.0 2.5 %collective-permute-start.10 = (f32[9,24,128]{2,1,0:T(8,128)S(1)}, f32[9,24,128]{2,1,0:T(8,128)S(1)}, u32[]{:S(2)}, u32[]{:S(2)}) collective-permute-start(f32[9,24,128]{2,1,0:T(8,128)S(1)} %pad_maximum_fusion.1.refs_4_), channel_id=1, source_target_pairs={{0,8},{1,9},{2,10},{3,11},{4,12},{5,13},{6,14},{7,15},{8,0},{9,1},... | collective-permute-start | bytes 331784 | tf_op jit(solution)/shard_map/ppermute | solution.py:177
  28.2 1.3 %collective-permute-start.11 = (f32[9,24,128]{2,1,0:T(8,128)S(1)}, f32[9,24,128]{2,1,0:T(8,128)S(1)}, u32[]{:S(2)}, u32[]{:S(2)}) collective-permute-start(f32[9,24,128]{2,1,0:T(8,128)S(1)} %collective-permute-done.9.refs_5_), channel_id=1, source_target_pairs={{0,8},{1,9},{2,10},{3,11},{4,12},{5,13},{6,14},{7,15},{8,0},{9,1},... | collective-permute-start | bytes 331784 | tf_op jit(solution)/shard_map/ppermute | solution.py:177
